TPU v7x, 32 devices: a whole 2x2x4 slice. The times are simulated.
32 devices in a mesh: freq: 4 (over y, x), rows: 8 (over z, core).
Axes of the slice: x: 2, y: 2, z: 4, core: 2. Of those that a mesh axis runs over, the one named last changes fastest.
Arguments:
- coupling: bfloat16 [8192, 8192], P('rows'), may hold values from -1 to 1
- delays: int32 [8192, 8192], P('rows'), may hold values from 0 to 63
- freq_index: int32 [4], P('freq'), parts along dimension 0, may hold values from 0 to 255
- initial: float32 [4, 2, 8192], P('freq', None, 'rows'), parts along dimension 0, may hold values from -6 to 6
Outputs:
- eigvector: float32 [4, 2, 8192], P('freq', None, 'rows'), parts along dimension 0
- eigvalue: float32 [4, 2], P('freq'), parts along dimension 0
There are 4 independent parts, one for each index of `freq`. A program takes and returns all parts, laid end to end along the dimension named above; an argument that names none is the same for every part. Nothing has to cross between parts.
All inputs are finite; a program needn't handle non-finite values.
Results may differ from a plain program's by a relative error of at most 0.0003.
Values sent between devices are 32-bit elements; how exact they have to be, the bound alone decides.
No kernel may reach another device: no remote copies, remote signals or barrier semaphores. Data moves between devices by JAX's collectives and lax.ppermute only.
A program may use at most 192 MiB of HBM per device.

v0:
```python
import math
import jax
import jax.numpy as jnp
from jax import lax
from jax.sharding import PartitionSpec as P

N = 8192
FTOTAL = 256
ITERS = 4
EPS = 1e-06


def build_operator(coupling, delays, which_freq):
    step_count = which_freq + 1
    residue = jnp.remainder(step_count * delays, 2 * FTOTAL)
    phase_angle = residue.astype(jnp.float32) * (math.pi / FTOTAL)
    weights = coupling.astype(jnp.float32)
    real_part = -weights * jnp.cos(phase_angle)
    imag_part = weights * jnp.sin(phase_angle)
    angular = step_count.astype(jnp.float32) * (math.pi / FTOTAL)
    return (real_part, imag_part, angular)


def product(real_part, imag_part, angular, gathered, own_rows):
    real_prod = jnp.dot(
        real_part, gathered.T, precision=lax.Precision.HIGHEST, preferred_element_type=jnp.float32
    )
    imag_prod = jnp.dot(
        imag_part, gathered.T, precision=lax.Precision.HIGHEST, preferred_element_type=jnp.float32
    )
    new_real = real_prod[:, 0] - imag_prod[:, 1] - angular * own_rows[1]
    new_imag = real_prod[:, 1] + imag_prod[:, 0] + angular * own_rows[0]
    return jnp.stack([new_real, new_imag], axis=0)


def power(coupling, delays, indices, first):
    real_all, imag_all, angular_all = lax.map(
        lambda which: build_operator(coupling, delays, which), indices
    )
    iterate = first
    previous_whole = first
    whole_iterate = first
    divisor = jnp.ones((first.shape[0], 1, 1), jnp.float32)
    for sweep in range(ITERS + 1):
        whole_iterate = lax.all_gather(iterate, "rows", axis=2, tiled=True)
        squares = jnp.sum(whole_iterate * whole_iterate, axis=(1, 2))
        divisor = jnp.sqrt(squares / N + EPS)[:, None, None]
        if sweep < ITERS:
            normed = iterate / divisor
            previous_whole = whole_iterate / divisor
            iterate = lax.map(
                lambda packed: product(packed[0], packed[1], packed[2], packed[3], packed[4]),
                (real_all, imag_all, angular_all, previous_whole, normed),
            )
    dot_real = jnp.sum(
        previous_whole[:, 0] * whole_iterate[:, 0] + previous_whole[:, 1] * whole_iterate[:, 1],
        axis=1,
    )
    dot_imag = jnp.sum(
        previous_whole[:, 0] * whole_iterate[:, 1] - previous_whole[:, 1] * whole_iterate[:, 0],
        axis=1,
    )
    result = iterate / divisor
    estimate = jnp.stack([dot_real, dot_imag], axis=1) / N
    return (result, estimate)


def shards(coupling, delays, freq_index, initial):

    def visit(carry, packed):
        which_freq, first = packed
        result, estimate = power(coupling, delays, which_freq[None], first[None])
        return (carry, (result[0], estimate[0]))

    unused, outputs = lax.scan(visit, jnp.int32(0), (freq_index, initial))
    eigvector, eigvalue = outputs
    return (eigvector, eigvalue)


def solution(mesh):
    return jax.shard_map(
        shards,
        mesh=mesh,
        in_specs=(P("rows", None), P("rows", None), P("freq"), P("freq", None, "rows")),
        out_specs=(P("freq", None, "rows"), P("freq", None)),
        check_vma=False,
    )
```

profile of v0, /device:TPU:0, one launch (start us, length us, event | category | flops | bytes accessed | tf_op | source)
XLA Modules:
  0.0 478.9 jit_solution(772224042721452039)
XLA Ops:
  1.3 15.9 %all_gather.20 = f32[1,2,8192]{2,1,0:T(2,128)S(1)} all-gather(f32[1,2,1024]{2,1,0:T(2,128)} %param.7), channel_id=1, replica_groups=mesh['freq'=4,'rows'=8] {'rows'}, dimensions={2}, use_global_device_ids=true | all-gather | bytes 73728 | tf_op jit(solution)/shard_map/while/body/eval_jaxpr/all_gather | solution.py:45
  17.2 0.7 multiply_reduce_fusion.4
  18.5 0.7 broadcast_divide_fusion.4
  19.3 138.6 %fusion = (f32[1024,8192]{1,0:T(8,128)}, f32[1024,8192]{1,0:T(8,128)}) fusion(bf16[1024,8192]{1,0:T(8,128)(2,1)} %param.4, s32[1024,8192]{1,0:T(8,128)} %param.5, s32[]{:T(128)} %bitcast), kind=kLoop, calls=%fused_computation.5 | loop fusion | flops 150994944 | bytes 117440512 | tf_op jit(solution)/shard_map/while/body/eval_jaxpr/while/body/eval_jaxpr/mul | solution.py:18
  157.8 31.9 %fusion.6 = f32[1024,2]{0,1:T(2,128)S(1)} fusion(f32[1024,8192]{1,0:T(8,128)} %get-tuple-element.181, f32[1,2,8192]{2,1,0:T(2,128)S(1)} %all_gather.20, f32[]{:T(128)S(6)} %sqrt.25), kind=kOutput, calls=%fused_computation.11 | convolution fusion | flops 201342976 | bytes 33628164 | tf_op jit(solution)/shard_map/while/body/eval_jaxpr/while/body/eval_jaxpr/dot_general | solution.py:25
  189.7 32.0 %fusion.4 = f32[1024,2]{0,1:T(2,128)S(1)} fusion(f32[1024,8192]{1,0:T(8,128)} %get-tuple-element.182, f32[1,2,8192]{2,1,0:T(2,128)S(1)} %all_gather.20, f32[]{:T(128)S(6)} %sqrt.25), kind=kOutput, calls=%fused_computation.9 | convolution fusion | flops 201342976 | bytes 33628164 | tf_op jit(solution)/shard_map/while/body/eval_jaxpr/while/body/eval_jaxpr/dot_general | solution.py:28
  221.8 14.0 %all-gather = f32[2,8192]{1,0:T(2,128)S(1)} all-gather(f32[2,1024]{1,0:T(2,128)S(1)} %pad_maximum_fusion), channel_id=2, replica_groups=mesh['freq'=4,'rows'=8] {'rows'}, dimensions={1}, use_global_device_ids=true | all-gather | bytes 73728 | tf_op jit(solution)/shard_map/while/body/eval_jaxpr/all_gather | solution.py:45
  235.8 0.7 multiply_reduce_fusion.2
  237.1 32.1 %fusion.8 = f32[1024,2]{0,1:T(2,128)S(1)} fusion(f32[1024,8192]{1,0:T(8,128)} %get-tuple-element.181, f32[2,8192]{1,0:T(2,128)S(1)} %all-gather, f32[]{:T(128)S(6)} %sqrt.26), kind=kOutput, calls=%fused_computation.66 | convolution fusion | flops 201342976 | bytes 33628164 | tf_op jit(solution)/shard_map/while/body/eval_jaxpr/while/body/eval_jaxpr/dot_general | solution.py:25
  269.2 31.9 %fusion.9 = f32[1024,2]{0,1:T(2,128)S(1)} fusion(f32[1024,8192]{1,0:T(8,128)} %get-tuple-element.182, f32[2,8192]{1,0:T(2,128)S(1)} %all-gather, f32[]{:T(128)S(6)} %sqrt.26), kind=kOutput, calls=%fused_computation.67 | convolution fusion | flops 201342976 | bytes 33628164 | tf_op jit(solution)/shard_map/while/body/eval_jaxpr/while/body/eval_jaxpr/dot_general | solution.py:28
  301.2 14.0 %all-gather.1 = f32[2,8192]{1,0:T(2,128)S(1)} all-gather(f32[2,1024]{1,0:T(2,128)S(1)} %pad_maximum_fusion.1), channel_id=3, replica_groups=mesh['freq'=4,'rows'=8] {'rows'}, dimensions={1}, use_global_device_ids=true | all-gather | bytes 73728 | tf_op jit(solution)/shard_map/while/body/eval_jaxpr/all_gather | solution.py:45
  315.1 0.7 multiply_reduce_fusion.1
  316.5 32.3 %fusion.10 = f32[1024,2]{0,1:T(2,128)S(1)} fusion(f32[1024,8192]{1,0:T(8,128)} %get-tuple-element.181, f32[2,8192]{1,0:T(2,128)S(1)} %all-gather.1, f32[]{:T(128)S(6)} %sqrt.27), kind=kOutput, calls=%fused_computation.68 | convolution fusion | flops 201342976 | bytes 33628164 | tf_op jit(solution)/shard_map/while/body/eval_jaxpr/while/body/eval_jaxpr/dot_general | solution.py:25
  348.8 31.9 %fusion.11 = f32[1024,2]{0,1:T(2,128)S(1)} fusion(f32[1024,8192]{1,0:T(8,128)} %get-tuple-element.182, f32[2,8192]{1,0:T(2,128)S(1)} %all-gather.1, f32[]{:T(128)S(6)} %sqrt.27), kind=kOutput, calls=%fused_computation.69 | convolution fusion | flops 201342976 | bytes 33628164 | tf_op jit(solution)/shard_map/while/body/eval_jaxpr/while/body/eval_jaxpr/dot_general | solution.py:28
  380.8 14.0 %all-gather.2 = f32[2,8192]{1,0:T(2,128)S(1)} all-gather(f32[2,1024]{1,0:T(2,128)S(1)} %pad_maximum_fusion.2), channel_id=4, replica_groups=mesh['freq'=4,'rows'=8] {'rows'}, dimensions={1}, use_global_device_ids=true | all-gather | bytes 73728 | tf_op jit(solution)/shard_map/while/body/eval_jaxpr/all_gather | solution.py:45
  394.8 0.7 multiply_reduce_fusion
  396.1 32.0 %fusion.13 = f32[1024,2]{0,1:T(2,128)S(1)} fusion(f32[1024,8192]{1,0:T(8,128)} %get-tuple-element.182, f32[2,8192]{1,0:T(2,128)S(1)} %all-gather.2, f32[]{:T(128)S(6)} %sqrt.28), kind=kOutput, calls=%fused_computation.71 | convolution fusion | flops 201342976 | bytes 33628164 | tf_op jit(solution)/shard_map/while/body/eval_jaxpr/while/body/eval_jaxpr/dot_general | solution.py:28
  428.2 31.9 %fusion.12 = f32[1024,2]{0,1:T(2,128)S(1)} fusion(f32[1024,8192]{1,0:T(8,128)} %get-tuple-element.181, f32[2,8192]{1,0:T(2,128)S(1)} %all-gather.2, f32[]{:T(128)S(6)} %sqrt.28), kind=kOutput, calls=%fused_computation.70 | convolution fusion | flops 201342976 | bytes 33628164 | tf_op jit(solution)/shard_map/while/body/eval_jaxpr/while/body/eval_jaxpr/dot_general | solution.py:25
  460.2 14.0 %all-gather.3 = f32[2,8192]{1,0:T(2,128)S(1)} all-gather(f32[2,1024]{1,0:T(2,128)S(1)} %pad_maximum_fusion.3), channel_id=5, replica_groups=mesh['freq'=4,'rows'=8] {'rows'}, dimensions={1}, use_global_device_ids=true | all-gather | bytes 73728 | tf_op jit(solution)/shard_map/while/body/eval_jaxpr/all_gather | solution.py:45
  474.2 0.7 multiply_reduce_fusion.3
  475.5 0.6 maximum_divide_fusion.3
  476.1 0.8 add_reduce_fusion
  476.9 1.8 maximum_multiply_fusion
  (16 shorter events, 0.3 us)
where the time goes:
time: 486 us; the launch traced here: 479 us
  matrix products  256 us (53%)
  other arithmetic  146 us (30%)
  blocking collectives  71.9 us (15%)
  between operations  5.07 us (1%)
    mul x1, other arithmetic, build_operator(): real_part = -weights * jnp.cos(phase_angle)  139 us
    dot_general x4, matrix products, product(): jnp.dot(real_part, gathered.T, precision=lax.Precision.HIGHEST, preferred...  128 us
    dot_general x4, matrix products, product(): jnp.dot(imag_part, gathered.T, precision=lax.Precision.HIGHEST, preferred...  128 us
    all_gather x5, blocking collectives, power(): whole_iterate = lax.all_gather(iterate, 'rows', axis=2, tiled=True)  71.9 us

commit v1 on v0

--- a/solution.py
+++ b/solution.py
@@ -42,7 +42,7 @@
     whole_iterate = first
     divisor = jnp.ones((first.shape[0], 1, 1), jnp.float32)
     for sweep in range(ITERS + 1):
-        whole_iterate = lax.all_gather(iterate, "rows", axis=2, tiled=True)
+        whole_iterate = jnp.concatenate(lax.all_gather(iterate, "rows"), axis=2)
         squares = jnp.sum(whole_iterate * whole_iterate, axis=(1, 2))
         divisor = jnp.sqrt(squares / N + EPS)[:, None, None]
         if sweep < ITERS:

time: 486 us -> 485 us (level)
  no operation moved by 1% of the time
where the time goes in v1:
time: 485 us; the launch traced here: 478 us
  matrix products  255 us (53%)
  other arithmetic  146 us (30%)
  blocking collectives  71.9 us (15%)
  between operations  5.1 us (1%)
    mul x1, other arithmetic, build_operator(): real_part = -weights * jnp.cos(phase_angle)  139 us
    dot_general x4, matrix products, product(): jnp.dot(imag_part, gathered.T, precision=lax.Precision.HIGHEST, preferred...  128 us
    dot_general x4, matrix products, product(): jnp.dot(real_part, gathered.T, precision=lax.Precision.HIGHEST, preferred...  127 us
    all_gather x5, blocking collectives, power(): whole_iterate = jnp.concatenate(lax.all_gather(iterate, 'rows'), axis=2)  71.9 us

profile of v1, /device:TPU:0, one launch (start us, length us, event | category | flops | bytes accessed | tf_op | source)
XLA Modules:
  0.0 478.0 jit_solution(2556770175705546833)
XLA Ops:
  1.3 15.9 %all-gather = f32[8,2,1024]{2,1,0:T(2,128)S(1)} all-gather(f32[1,2,1024]{2,1,0:T(2,128)} %param.7), channel_id=2, replica_groups=mesh['freq'=4,'rows'=8] {'rows'}, dimensions={0}, use_global_device_ids=true | all-gather | bytes 73728 | tf_op jit(solution)/shard_map/while/body/eval_jaxpr/all_gather | solution.py:45
  17.2 0.7 multiply_reduce_fusion.3
  18.6 0.7 broadcast_divide_fusion.4
  19.3 138.6 %fusion = (f32[1024,8192]{1,0:T(8,128)}, f32[1024,8192]{1,0:T(8,128)}) fusion(bf16[1024,8192]{1,0:T(8,128)(2,1)} %param.4, s32[1024,8192]{1,0:T(8,128)} %param.5, s32[]{:T(128)} %bitcast), kind=kLoop, calls=%fused_computation.5 | loop fusion | flops 150994944 | bytes 117440512 | tf_op jit(solution)/shard_map/while/body/eval_jaxpr/while/body/eval_jaxpr/mul | solution.py:18
  157.8 31.7 %fusion.5 = f32[1024,2]{0,1:T(2,128)S(1)} fusion(f32[1024,8192]{1,0:T(8,128)} %get-tuple-element.181, f32[2,8192]{1,0:T(2,128)S(1)} %bitcast.116), kind=kOutput, calls=%fused_computation.63 | convolution fusion | flops 201326592 | bytes 33628160 | tf_op jit(solution)/shard_map/while/body/eval_jaxpr/while/body/eval_jaxpr/dot_general | solution.py:25
  189.6 31.9 %fusion.6 = f32[1024,2]{0,1:T(2,128)S(1)} fusion(f32[1024,8192]{1,0:T(8,128)} %get-tuple-element.182, f32[2,8192]{1,0:T(2,128)S(1)} %bitcast.117), kind=kOutput, calls=%fused_computation.64 | convolution fusion | flops 201326592 | bytes 33628160 | tf_op jit(solution)/shard_map/while/body/eval_jaxpr/while/body/eval_jaxpr/dot_general | solution.py:28
  221.6 14.0 %all-gather.5 = f32[8,2,1024]{2,1,0:T(2,128)S(1)} all-gather(f32[1,2,1024]{2,1,0:T(2,128)S(1)} %maximum_bitcast_fusion), channel_id=3, replica_groups=mesh['freq'=4,'rows'=8] {'rows'}, dimensions={0}, use_global_device_ids=true | all-gather | bytes 73728 | tf_op jit(solution)/shard_map/while/body/eval_jaxpr/all_gather | solution.py:45
  235.6 0.7 multiply_reduce_fusion.2
  237.0 32.0 %fusion.8 = f32[1024,2]{0,1:T(2,128)S(1)} fusion(f32[1024,8192]{1,0:T(8,128)} %get-tuple-element.182, f32[2,8192]{1,0:T(2,128)S(1)} %bitcast.118), kind=kOutput, calls=%fused_computation.66 | convolution fusion | flops 201326592 | bytes 33628160 | tf_op jit(solution)/shard_map/while/body/eval_jaxpr/while/body/eval_jaxpr/dot_general | solution.py:28
  268.9 31.7 %fusion.7 = f32[1024,2]{0,1:T(2,128)S(1)} fusion(f32[1024,8192]{1,0:T(8,128)} %get-tuple-element.181, f32[2,8192]{1,0:T(2,128)S(1)} %bitcast.119), kind=kOutput, calls=%fused_computation.65 | convolution fusion | flops 201326592 | bytes 33628160 | tf_op jit(solution)/shard_map/while/body/eval_jaxpr/while/body/eval_jaxpr/dot_general | solution.py:25
  300.7 14.0 %all-gather.6 = f32[8,2,1024]{2,1,0:T(2,128)S(1)} all-gather(f32[1,2,1024]{2,1,0:T(2,128)S(1)} %maximum_bitcast_fusion.1), channel_id=4, replica_groups=mesh['freq'=4,'rows'=8] {'rows'}, dimensions={0}, use_global_device_ids=true | all-gather | bytes 73728 | tf_op jit(solution)/shard_map/while/body/eval_jaxpr/all_gather | solution.py:45
  314.7 0.7 multiply_reduce_fusion.1
  316.1 32.2 %fusion.10 = f32[1024,2]{0,1:T(2,128)S(1)} fusion(f32[1024,8192]{1,0:T(8,128)} %get-tuple-element.182, f32[2,8192]{1,0:T(2,128)S(1)} %bitcast.120), kind=kOutput, calls=%fused_computation.68 | convolution fusion | flops 201326592 | bytes 33628160 | tf_op jit(solution)/shard_map/while/body/eval_jaxpr/while/body/eval_jaxpr/dot_general | solution.py:28
  348.3 31.7 %fusion.9 = f32[1024,2]{0,1:T(2,128)S(1)} fusion(f32[1024,8192]{1,0:T(8,128)} %get-tuple-element.181, f32[2,8192]{1,0:T(2,128)S(1)} %bitcast.121), kind=kOutput, calls=%fused_computation.67 | convolution fusion | flops 201326592 | bytes 33628160 | tf_op jit(solution)/shard_map/while/body/eval_jaxpr/while/body/eval_jaxpr/dot_general | solution.py:25
  380.1 14.0 %all-gather.7 = f32[8,2,1024]{2,1,0:T(2,128)S(1)} all-gather(f32[1,2,1024]{2,1,0:T(2,128)S(1)} %maximum_bitcast_fusion.2), channel_id=5, replica_groups=mesh['freq'=4,'rows'=8] {'rows'}, dimensions={0}, use_global_device_ids=true | all-gather | bytes 73728 | tf_op jit(solution)/shard_map/while/body/eval_jaxpr/all_gather | solution.py:45
  394.1 0.7 multiply_reduce_fusion
  395.5 31.9 %fusion.12 = f32[1024,2]{0,1:T(2,128)S(1)} fusion(f32[1024,8192]{1,0:T(8,128)} %get-tuple-element.182, f32[2,8192]{1,0:T(2,128)S(1)} %bitcast.113), kind=kOutput, calls=%fused_computation.70 | convolution fusion | flops 201326592 | bytes 33628160 | tf_op jit(solution)/shard_map/while/body/eval_jaxpr/while/body/eval_jaxpr/dot_general | solution.py:28
  427.4 31.7 %fusion.11 = f32[1024,2]{0,1:T(2,128)S(1)} fusion(f32[1024,8192]{1,0:T(8,128)} %get-tuple-element.181, f32[2,8192]{1,0:T(2,128)S(1)} %bitcast.114), kind=kOutput, calls=%fused_computation.69 | convolution fusion | flops 201326592 | bytes 33628160 | tf_op jit(solution)/shard_map/while/body/eval_jaxpr/while/body/eval_jaxpr/dot_general | solution.py:25
  459.2 14.0 %all-gather.8 = f32[8,2,1024]{2,1,0:T(2,128)S(1)} all-gather(f32[1,2,1024]{2,1,0:T(2,128)S(1)} %maximum_bitcast_fusion.3), channel_id=6, replica_groups=mesh['freq'=4,'rows'=8] {'rows'}, dimensions={0}, use_global_device_ids=true | all-gather | bytes 73728 | tf_op jit(solution)/shard_map/while/body/eval_jaxpr/all_gather | solution.py:45
  473.2 0.7 fusion.4
  474.6 0.6 maximum_divide_fusion.3
  475.2 0.8 add_reduce_fusion
  476.0 1.8 maximum_multiply_fusion
  (19 shorter events, 0.3 us)
